TPU v7x, 8 devices: a whole 2x2x1 slice. The times are simulated.
8 devices in a mesh: dp: 1 (over z), fsdp: 2 (over y), tp: 4 (over x, core).
Axes of the slice: x: 2, y: 2, z: 1, core: 2. Of those that a mesh axis runs over, the one named last changes fastest.
Arguments:
- hidden: bfloat16 [2048, 3072], P(('dp', 'fsdp', 'tp'))
- w_head: bfloat16 [3072, 128256], P('fsdp', 'tp')
- labels: int32 [2048], P(('dp', 'fsdp', 'tp'))
Outputs:
- output 1: float32 [1], P('dp')
- output 2: bfloat16 [2048, 3072], P(('dp', 'fsdp', 'tp'))
- output 3: bfloat16 [3072, 128256], P(('dp', 'fsdp'), 'tp')
All inputs are finite; a program needn't handle non-finite values.
Results may differ from a plain program's by a relative error of at most 0.001.
Values are sent between devices in bfloat16 or wider.
A program may use at most 1 GiB of HBM per device.

v0:
```python
import jax
import jax.numpy as jnp
from jax import lax
from jax.sharding import PartitionSpec as P


def solution(mesh):
    fsdp_size = mesh.shape["fsdp"]
    tp_size = mesh.shape["tp"]
    token_spec = P(("dp", "fsdp", "tp"), None)
    label_spec = P(("dp", "fsdp", "tp"))

    def local_step(hidden, w_head, labels):
        rows_dev = hidden.shape[0]
        vocab_dev = w_head.shape[1]
        inv_tokens = 1.0 / (rows_dev * tp_size * fsdp_size)
        w_full = lax.all_gather(w_head, "fsdp", axis=0, tiled=True)
        x_full = lax.all_gather(hidden, "tp", axis=0, tiled=True)
        lab_full = lax.all_gather(labels, "tp", axis=0, tiled=True)
        logits = jnp.dot(x_full, w_full, preferred_element_type=jnp.float32)
        row_max = lax.pmax(jnp.max(logits, axis=1), "tp")
        exp_rows = jnp.exp(logits - row_max[:, None])
        local_ids = lab_full - lax.axis_index("tp") * vocab_dev
        onehot = local_ids[:, None] == jnp.arange(vocab_dev, dtype=jnp.int32)[None, :]
        local_stats = jnp.stack([jnp.sum(exp_rows, axis=1), jnp.sum(jnp.where(onehot, logits, 0.0), axis=1)])
        stat_sums = lax.psum(local_stats, "tp")
        row_sum = stat_sums[0]
        target = stat_sums[1]
        tok_loss = row_max + jnp.log(row_sum) - target
        mean_loss = lax.psum(jnp.sum(tok_loss), "fsdp") * inv_tokens
        prob_rows = exp_rows / row_sum[:, None]
        grad_logits = (jnp.where(onehot, prob_rows - 1.0, prob_rows) * inv_tokens).astype(jnp.bfloat16)
        d_x_part = jnp.einsum("tv,hv->th", grad_logits, w_full, preferred_element_type=jnp.float32)
        d_hidden = lax.psum_scatter(d_x_part, "tp", scatter_dimension=0, tiled=True).astype(jnp.bfloat16)
        d_w_part = jnp.einsum("th,tv->hv", x_full, grad_logits, preferred_element_type=jnp.float32)
        d_w_head = lax.psum_scatter(d_w_part, "fsdp", scatter_dimension=0, tiled=True).astype(jnp.bfloat16)
        return mean_loss.reshape(1), d_hidden, d_w_head

    return jax.shard_map(
        local_step,
        mesh=mesh,
        in_specs=(token_spec, P("fsdp", "tp"), label_spec),
        out_specs=(P("dp"), token_spec, P(("dp", "fsdp"), "tp")),
        check_vma=False,
    )
```

profile of v0, /device:TPU:0, one launch (start us, length us, event | category | flops | bytes accessed | tf_op | source)
XLA Modules:
  0.0 7359.1 jit_solution(14117745826544460407)
XLA Ops:
  7.2 0.0 all-gather.4.cloned.1.call-start
  7.2 0.7 all-gather.4.cloned.1.call-update
  7.9 0.0 all-gather.6.cloned.1.call-start
  7.9 0.7 all-gather.6.cloned.1.call-update
  8.6 0.0 reduce-scatter.3.cloned.1.call-start
  8.7 9.8 all-gather
  18.5 0.6 broadcast_subtract_fusion
  19.1 36.9 all-gather.4.cloned.1.call-done
  56.0 2227.5 %all-gather.6.cloned.1.call-done = bf16[3072,32064]{0,1:T(8,128)(2,1)} async-done(((bf16[1536,32064]{0,1:T(8,128)(2,1)}), bf16[3072,32064]{0,1:T(8,128)(2,1)}) %all-gather.6.cloned.1.call-update) | async-done | bytes 197001232 | tf_op jit(solution)/shard_map/all_gather | solution.py:17
  2283.5 218.6 %fusion.7 = (f32[1024]{0:T(1024)S(1)}, f32[1024,32064]{0,1:T(8,128)}) fusion(bf16[1024,3072]{1,0:T(8,128)(2,1)} %all-gather.4.cloned.1.call-done, bf16[3072,32064]{0,1:T(8,128)(2,1)} %all-gather.6.cloned.1.call-done), kind=kOutput, calls=%fused_computation.13 | convolution fusion | flops 201762078720 | bytes 334630912 | tf_op jit(solution)/shard_map/dot_general | solution.py:20
  2502.1 6.3 pmax.7
  2508.3 40.5 fusion.2
  2548.9 6.2 psum.14
  2555.1 0.6 fusion.6
  2555.7 242.9 %fusion.4 = f32[1024,3072]{1,0:T(8,128)} fusion(bf16[3072,32064]{0,1:T(8,128)(2,1)} %all-gather.6.cloned.1.call-done, f32[1024,32064]{0,1:T(8,128)} %get-tuple-element.8, f32[1024]{0:T(1024)S(1)} %bitcast.21, s32[1024]{0:T(1024)S(1)} %bitcast.17, f32[1024]{0:T(1024)S(1)} %pmax.7), kind=kOutput, calls=%fused_computation.11 | convolution fusion | flops 201959079936 | bytes 340930560 | tf_op jit(solution)/shard_map/tv,hv->th/dot_general | solution.py:33
  2798.6 0.3 reduce-scatter.5.cloned.1.call-start
  2798.9 231.4 %convolution_bitcast_fusion = f32[3072,32064]{0,1:T(8,128)} fusion(bf16[1024,3072]{1,0:T(8,128)(2,1)} %all-gather.4.cloned.1.call-done, f32[1024,32064]{0,1:T(8,128)} %get-tuple-element.8, f32[1024]{0:T(1024)S(1)} %bitcast.22, s32[1024]{0:T(1024)S(1)} %bitcast.18, f32[1024]{0:T(1024)S(1)} %pmax.7), kind=kOutput, calls=%fused_computation | convolution fusion | flops 201959079936 | bytes 531640320 | tf_op jit(solution)/shard_map/th,tv->hv/dot_general | solution.py:35
  3030.3 0.7 copy-done.1
  3030.9 0.6 subtract_reduce_fusion
  3031.5 5.6 psum.15
  3037.8 0.0 reduce-scatter.3.cloned.1.call-done
  3037.8 3.3 convert_element_type.10
  3041.1 4217.7 %reduce-scatter.5.cloned.1.call-done = f32[1536,32064]{0,1:T(8,128)} async-done(((f32[3072,32064]{0,1:T(8,128)}), f32[1536,32064]{0,1:T(8,128)}) %reduce-scatter.5.cloned.1.call-update) | async-done | bytes 197001232 | tf_op jit(solution)/shard_map/reduce_scatter | solution.py:36
  7258.8 92.7 %convert_element_type.11 = bf16[1536,32064]{0,1:T(8,128)(2,1)} convert(f32[1536,32064]{0,1:T(8,128)} %reduce-scatter.5.cloned.1.call-done) | non-fusion elementwise | flops 49250304 | bytes 295501824 | tf_op jit(solution)/shard_map/convert_element_type | solution.py:36
  (6 shorter events, 0.1 us)
Async XLA Ops:
  7.2 48.8 all-gather.4.cloned.1.call-start
  7.9 2275.6 %all-gather.6.cloned.1.call-start = ((), (), s32[]{:S(2)}) async-start(), calls=%async_computation.3 | async-start | bytes 295501824 | tf_op jit(solution)/shard_map/all_gather | solution.py:17
  8.6 3029.2 %reduce-scatter.3.cloned.1.call-start = ((), (), s32[]{:S(2)}) async-start(), calls=%async_computation.4 | async-start | bytes 15728640 | tf_op jit(solution)/shard_map/reduce_scatter | solution.py:34
  2283.5 224.9 %copy-start = (s32[4,1,256]{2,1,0:T(1,128)S(1)}, s32[4,1,256]{2,1,0:T(1,128)}, u32[]{:S(2)}) copy-start(s32[4,1,256]{2,1,0:T(1,128)} %broadcast_subtract_fusion) | copy-start | bytes 12292
  2798.6 4460.1 %reduce-scatter.5.cloned.1.call-start = ((), (), s32[]{:S(2)}) async-start(), calls=%async_computation.5 | async-start | bytes 591003648 | tf_op jit(solution)/shard_map/reduce_scatter | solution.py:36
  3030.2 0.7 copy-start.1
Sparse Core Ops, SparseCore 0:
  9.5 46.4 all-gather.3
  57.5 2225.9 all-gather.5
  2798.7 90.0 reduce-scatter.2
  3030.4 4228.3 reduce-scatter.4
where the time goes:
time: 7360 us
  waiting for transfers between devices  6480 us (88%)
  matrix products  693 us (9%)
  other arithmetic  138 us (2%)
    reduce_scatter x1, waiting for transfers between devices, local_step(): lax.psum_scatter(d_w_part, 'fsdp', scatter_dimension=0, tiled=True)  4220 us
    all_gather x1, waiting for transfers between devices, local_step(): w_full = lax.all_gather(w_head, 'fsdp', axis=0, tiled=True)  2230 us
    dot_general x1, matrix products, local_step(): jnp.einsum('tv,hv->th', grad_logits, w_full, preferred_element_type=jnp.f...  243 us
    dot_general x1, matrix products, local_step(): jnp.einsum('th,tv->hv', x_full, grad_logits, preferred_element_type=jnp.f...  231 us
    dot_general x1, matrix products, local_step(): logits = jnp.dot(x_full, w_full, preferred_element_type=jnp.float32)  219 us
  transfers between devices with their start and end apart: 4, of which 3 were waited for; matrix products, arithmetic and copies ran while one was open for 3% of the time, Pallas kernels for 0%

commit v1 on v0

v1 whole, which is shorter than its diff:
```python
import jax
import jax.numpy as jnp
from jax import lax
from jax.experimental import pallas as pl
from jax.experimental.pallas import tpu as pltpu
from jax.sharding import PartitionSpec as P


CHUNKS = (384, 1152, 2560, 2560, 2560, 2560, 2560, 1312, 384)
SWAP = [(0, 1), (1, 0)]


def _place_body(start_ref, *refs):
    piece, out, sem = refs[-3], refs[-2], refs[-1]
    rows = piece.shape[0]
    start = pl.multiple_of(start_ref[0] + pl.program_id(0) * rows, 16)
    copy = pltpu.make_async_copy(piece, out.at[pl.ds(start, rows)], sem)
    copy.start()
    copy.wait()


def place(out, piece, start, shape, rows):
    n, cols = piece.shape
    in_specs = [pl.BlockSpec((rows, cols), lambda i, start: (i, 0))]
    args = [piece]
    aliases = {}
    if out is not None:
        in_specs = [pl.BlockSpec(memory_space=pl.ANY)] + in_specs
        args = [out, piece]
        aliases = {1: 0}
    return pl.pallas_call(
        _place_body,
        out_shape=jax.ShapeDtypeStruct(shape, piece.dtype),
        grid_spec=pltpu.PrefetchScalarGridSpec(
            num_scalar_prefetch=1,
            grid=(n // rows,),
            in_specs=in_specs,
            out_specs=pl.BlockSpec(memory_space=pl.ANY),
            scratch_shapes=[pltpu.SemaphoreType.DMA],
        ),
        input_output_aliases=aliases,
        cost_estimate=pl.CostEstimate(flops=n * cols * 4, bytes_accessed=4 * n * cols, transcendentals=0),
        name="place",
    )(jnp.reshape(start, (1,)).astype(jnp.int32), *args)


def dot_f32(a, b, contract):
    return lax.dot_general(a, b, (contract, ((), ())), preferred_element_type=jnp.float32)


def solution(mesh):
    fsdp_size = mesh.shape["fsdp"]
    tp_size = mesh.shape["tp"]
    token_spec = P(("dp", "fsdp", "tp"), None)
    label_spec = P(("dp", "fsdp", "tp"))

    def inner(hidden, w_head, labels):
        rows_dev = hidden.shape[0]
        rows_w, vocab_dev = w_head.shape
        half = vocab_dev // 2
        tokens = rows_dev * tp_size * fsdp_size
        inv_tokens = 1.0 / tokens
        f = lax.axis_index("fsdp")
        is0 = f == 0
        n_chunks = len(CHUNKS)
        offs = [sum(CHUNKS[:k]) for k in range(n_chunks)]

        def swap(a):
            return lax.ppermute(a, "fsdp", SWAP)

        def pick(a, b):
            return jnp.where(is0, a, b)

        hid_peer = swap(hidden)
        lab_peer = swap(labels)
        hid2 = jnp.concatenate([pick(hidden, hid_peer), pick(hid_peer, hidden)], axis=0)
        lab2 = jnp.concatenate([pick(labels, lab_peer), pick(lab_peer, labels)], axis=0)
        lab = lax.all_gather(lab2, "tp", axis=0, tiled=True)
        x_full = lax.all_gather(hid2, "tp", axis=0, tiled=True)
        x_lo, x_hi = x_full[:, :rows_w], x_full[:, rows_w:]
        x_own, x_oth = pick(x_lo, x_hi), pick(x_hi, x_lo)

        wt = w_head.T
        oth = []
        for k, width in enumerate(CHUNKS):
            lo, hi = wt[offs[k] : offs[k] + width], wt[half + offs[k] : half + offs[k] + width]
            oth.append(swap(pick(hi, lo)))
        own = pick(wt[:half], wt[half:])

        ids0 = lab - lax.axis_index("tp") * vocab_dev - f * half

        def onehot(off, width):
            return (ids0 - off)[None, :] == jnp.arange(width, dtype=jnp.int32)[:, None]

        z_own = dot_f32(own, x_own, ((1,), (1,)))
        zs, m, s, t = [], None, None, None
        for k, width in enumerate(CHUNKS):
            head = oth[k]
            if k > 0:
                head, s, t = lax.optimization_barrier((head, s, t))
            z = z_own[offs[k] : offs[k] + width] + dot_f32(head, x_oth, ((1,), (1,)))
            z_max = jnp.max(z, axis=0)
            m_new = z_max if m is None else jnp.maximum(m, z_max)
            s_new = jnp.sum(jnp.exp(z - m_new[None, :]), axis=0)
            t_new = jnp.sum(jnp.where(onehot(offs[k], width), z, 0.0), axis=0)
            s = s_new if m is None else s * jnp.exp(m - m_new) + s_new
            t = t_new if m is None else t + t_new
            m = m_new
            zs.append(z)
        stats = lax.all_gather(jnp.stack([m, s, t]), ("fsdp", "tp"), axis=0)
        row_max = jnp.max(stats[:, 0], axis=0)
        row_sum = jnp.sum(stats[:, 1] * jnp.exp(stats[:, 0] - row_max[None, :]), axis=0)
        target = jnp.sum(stats[:, 2], axis=0)
        tok_loss = row_max + jnp.log(row_sum) - target
        mean_loss = jnp.sum(tok_loss) * inv_tokens

        gs, recv, part = [], [], None
        for k, width in enumerate(CHUNKS):
            z = zs[k]
            if part is not None:
                z, _ = lax.optimization_barrier((z, part))
            prob = jnp.exp(z - row_max[None, :]) / row_sum[None, :]
            g = (jnp.where(onehot(offs[k], width), prob - 1.0, prob) * inv_tokens).astype(jnp.bfloat16)
            part = dot_f32(g, x_oth, ((1,), (0,))).astype(jnp.bfloat16)
            recv.append(swap(part))
            gs.append(g)

        gs, oth, _ = lax.optimization_barrier((gs, oth, part))
        g_all = jnp.concatenate(gs, axis=0)
        oth_all = jnp.concatenate(oth, axis=0)
        dx_own = dot_f32(g_all, own, ((0,), (0,)))
        rs_own = lax.psum_scatter(dx_own, "tp", scatter_dimension=0, tiled=True)
        dx_oth = dot_f32(g_all, oth_all, ((0,), (0,)))
        rs_oth = lax.psum_scatter(dx_oth, "tp", scatter_dimension=0, tiled=True)
        dw_own = dot_f32(g_all, x_own, ((1,), (0,))).astype(jnp.bfloat16)

        def mine(a):
            return pick(a[:rows_dev], a[rows_dev:])

        def theirs(a):
            return pick(a[rows_dev:], a[:rows_dev])

        back_own = swap(theirs(rs_own))
        back_oth = swap(theirs(rs_oth))
        d_own = mine(rs_own) + back_oth
        d_oth = mine(rs_oth) + back_own
        d_hidden = jnp.concatenate([pick(d_own, d_oth), pick(d_oth, d_own)], axis=1).astype(jnp.bfloat16)

        shape = (vocab_dev, rows_w)
        out = place(None, dw_own, f * half, shape, half // 6)
        for k, width in enumerate(CHUNKS):
            rows = width if width <= 512 else width // 2
            out = place(out, recv[k], (1 - f) * half + offs[k], shape, rows)
        return mean_loss.reshape(1), d_hidden, out.T

    return jax.shard_map(
        inner,
        mesh=mesh,
        in_specs=(token_spec, P("fsdp", "tp"), label_spec),
        out_specs=(P("dp"), token_spec, P(("dp", "fsdp"), "tp")),
        check_vma=False,
    )
```

time: 7360 us -> 2940 us (0.40)
  waiting for transfers between devices: 6480 us -> 1720 us
  local copies, waits for them, and re-layouts: 1.27 us -> 118 us
  matrix products: 693 us -> 771 us
  Pallas kernels: 0 us -> 75.8 us
    reduce_scatter x2, waiting for transfers between devices: 4220 us -> 0.01 us  [the longest x1 0.01 us: inner(): rs_oth = lax.psum_scatter(dx_oth, 'tp', scatter_dimension=0, tiled=True)]
    all_gather x2 -> x1, waiting for transfers between devices: 2260 us -> 0.01 us  [inner(): x_full = lax.all_gather(hid2, 'tp', axis=0, tiled=True)]
    ppermute x0 -> x22, waiting for transfers between devices: none -> 1720 us  [swap(): return lax.ppermute(a, 'fsdp', SWAP)]
    unnamed x4 -> x154, local copies, waits for them, and re-layouts: 0.67 us -> 115 us
    dot_general x3 -> x22, matrix products: 693 us -> 771 us  [dot_f32(): lax.dot_general(a, b, (contract, ((), ())), preferred_element_type=jnp.fl...]
    pallas_call x0 -> x10, Pallas kernels: none -> 75.8 us  [place(): pl.pallas_call(_place_body, out_shape=jax.ShapeDtypeStruct(shape, piece.d...]
  transfers between devices with their start and end apart: 4 -> 25, of which waited for: 3 -> 11; matrix products, arithmetic and copies ran while one was open for 3% -> 22% of each run, Pallas kernels for 0% -> 3%
where the time goes in v1:
time: 2940 us; the launch traced here: 2930 us
  waiting for transfers between devices  1720 us (59%)
  matrix products  771 us (26%)
  other arithmetic  192 us (7%)
  local copies, waits for them, and re-layouts  118 us (4%)
  Pallas kernels  75.8 us (3%)
    ppermute x22, waiting for transfers between devices, swap(): return lax.ppermute(a, 'fsdp', SWAP)  1720 us
    dot_general x22, matrix products, dot_f32(): lax.dot_general(a, b, (contract, ((), ())), preferred_element_type=jnp.fl...  771 us
    unnamed x154, local copies, waits for them, and re-layouts  115 us
    pallas_call x10, Pallas kernels, place(): pl.pallas_call(_place_body, out_shape=jax.ShapeDtypeStruct(shape, piece.d...  75.8 us
    select_n x9, other arithmetic, pick(): return jnp.where(is0, a, b)  68.8 us
  transfers between devices with their start and end apart: 25, of which 11 were waited for; matrix products, arithmetic and copies ran while one was open for 22% of the time, Pallas kernels for 3%

profile of v1, /device:TPU:0, one launch (start us, length us, event | category | flops | bytes accessed | tf_op | source)
XLA Modules:
  0.0 2934.8 jit_solution(4889409283550141525)
XLA Ops:
  10.6 34.6 %collective-permute-done = bf16[256,3072]{1,0:T(8,128)(2,1)S(1)} collective-permute-done((bf16[256,3072]{1,0:T(8,128)(2,1)}, bf16[256,3072]{1,0:T(8,128)(2,1)S(1)}, u32[]{:S(2)}, u32[]{:S(2)}) %collective-permute-start) | collective-permute-done | bytes 1572896 | tf_op jit(solution)/shard_map/ppermute | solution.py:69
  62.0 38.7 %slice_select_fusion.5 = (bf16[2560,1536]{1,0:T(8,128)(2,1)}, bf16[2560,1536]{1,0:T(8,128)(2,1)}, bf16[2560,1536]{1,0:T(8,128)(2,1)}, bf16[2560,1536]{1,0:T(8,128)(2,1)}, bf16[2560,1536]{1,0:T(8,128)(2,1)}) fusion(bf16[32064,1536]{1,0:T(8,128)(2,1)} %bitcast, pred[]{:T(512)S(6)} %eq.56), kind=kLoop, calls=%fused_computation.60 | loop fusion | flops 19660800 | bytes 117964800 | tf_op jit(solution)/shard_map/jit(_where)/select_n | solution.py:72
  110.0 226.9 %collective-permute-done.3 = s32[256]{0:T(256)S(1)} collective-permute-done((s32[256]{0:T(256)S(1)}, s32[256]{0:T(256)S(1)}, u32[]{:S(2)}, u32[]{:S(2)}) %collective-permute-start.3) | collective-permute-done | bytes 1056 | tf_op jit(solution)/shard_map/ppermute | solution.py:69
  348.2 115.9 %fusion.15 = f32[16032,2048]{1,0:T(8,128)} fusion(bf16[32064,1536]{1,0:T(8,128)(2,1)} %bitcast, pred[]{:T(512)S(6)} %eq.56, bf16[2048,3072]{1,0:T(8,128)(2,1)} %all-gather.5.cloned.1.call-done), kind=kOutput, calls=%fused_computation.64 | convolution fusion | flops 100892393472 | bytes 242418688 | tf_op jit(solution)/shard_map/dot_general | solution.py:48
  496.3 26.3 fusion.27
  532.7 277.6 %collective-permute-done.5 = bf16[2560,1536]{1,0:T(8,128)(2,1)} collective-permute-done((bf16[2560,1536]{1,0:T(8,128)(2,1)}, bf16[2560,1536]{1,0:T(8,128)(2,1)}, u32[]{:S(2)}, u32[]{:S(2)}) %collective-permute-start.5) | collective-permute-done | bytes 7864352 | tf_op jit(solution)/shard_map/ppermute | solution.py:69
  810.8 26.1 fusion.28
  847.0 131.8 %collective-permute-done.6 = bf16[2560,1536]{1,0:T(8,128)(2,1)} collective-permute-done((bf16[2560,1536]{1,0:T(8,128)(2,1)}, bf16[2560,1536]{1,0:T(8,128)(2,1)}, u32[]{:S(2)}, u32[]{:S(2)}) %collective-permute-start.6) | collective-permute-done | bytes 7864352 | tf_op jit(solution)/shard_map/ppermute | solution.py:69
  978.9 26.4 fusion.29
  1015.3 129.2 %collective-permute-done.7 = bf16[2560,1536]{1,0:T(8,128)(2,1)} collective-permute-done((bf16[2560,1536]{1,0:T(8,128)(2,1)}, bf16[2560,1536]{1,0:T(8,128)(2,1)}, u32[]{:S(2)}, u32[]{:S(2)}) %collective-permute-start.7) | collective-permute-done | bytes 7864352 | tf_op jit(solution)/shard_map/ppermute | solution.py:69
  1144.5 26.1 fusion.30
  1180.7 26.2 fusion.31
  1375.6 22.4 convolution_convert_fusion.2
  1406.2 22.4 convolution_convert_fusion.1
  1564.2 114.6 %fusion.34 = f32[2048,1536]{1,0:T(8,128)} fusion(bf16[16032,2048]{1,0:T(8,128)(2,1)} %constant_dynamic-update-slice_fusion, bf16[16032,1536]{1,0:T(8,128)(2,1)} %constant_dynamic-update-slice_fusion.9), kind=kOutput, calls=%fused_computation.154 | convolution fusion | flops 100864622592 | bytes 127500288 | tf_op jit(solution)/shard_map/dot_general | solution.py:48
  1678.8 119.9 %fusion.14 = f32[2048,1536]{1,0:T(8,128)} fusion(bf16[16032,2048]{1,0:T(8,128)(2,1)} %constant_dynamic-update-slice_fusion, bf16[32064,1536]{1,0:T(8,128)(2,1)} %bitcast, pred[]{:T(512)S(6)} %eq.56), kind=kOutput, calls=%fused_computation.63 | convolution fusion | flops 100889247744 | bytes 176750592 | tf_op jit(solution)/shard_map/dot_general | solution.py:48
  1803.7 695.4 %collective-permute-done.13.refs_1_ = bf16[384,1536]{1,0:T(8,128)(2,1)} collective-permute-done((bf16[384,1536]{1,0:T(8,128)(2,1)S(1)}, bf16[384,1536]{1,0:T(8,128)(2,1)}, u32[]{:S(2)}, u32[]{:S(2)}) %collective-permute-start.13) | collective-permute-done | bytes 1179680 | tf_op jit(solution)/shard_map/ppermute | solution.py:69
  2506.1 69.7 %collective-permute-done.14.refs_1_ = bf16[1152,1536]{1,0:T(8,128)(2,1)S(1)} collective-permute-done((bf16[1152,1536]{1,0:T(8,128)(2,1)}, bf16[1152,1536]{1,0:T(8,128)(2,1)S(1)}, u32[]{:S(2)}, u32[]{:S(2)}) %collective-permute-start.14) | collective-permute-done | bytes 3538976 | tf_op jit(solution)/shard_map/ppermute | solution.py:69
  2580.3 112.8 %convolution_convert_fusion.refs_0_ = bf16[16032,1536]{1,0:T(8,128)(2,1)} fusion(bf16[16032,2048]{1,0:T(8,128)(2,1)} %constant_dynamic-update-slice_fusion, pred[]{:T(512)S(6)} %eq.56, bf16[2048,3072]{1,0:T(8,128)(2,1)} %all-gather.5.cloned.1.call-done), kind=kOutput, calls=%fused_computation | convolution fusion | flops 100892393472 | bytes 127500288 | tf_op jit(solution)/shard_map/dot_general | solution.py:48
  2694.4 33.1 %place.10.refs_0_ = bf16[32064,1536]{1,0:T(8,128)(2,1)} custom-call(s32[1]{0:T(128)} %bitcast.18.start_ref, bf16[16032,1536]{1,0:T(8,128)(2,1)} %convolution_convert_fusion.refs_0_), custom_call_target="tpu_custom_call" | custom-call | flops 98500608 | bytes 98500608 | tf_op jit(solution)/shard_map/place/pallas_call | solution.py:31
  2763.7 70.8 %collective-permute-done.20.refs_1_ = bf16[1312,1536]{1,0:T(8,128)(2,1)} collective-permute-done((bf16[1312,1536]{1,0:T(8,128)(2,1)}, bf16[1312,1536]{1,0:T(8,128)(2,1)}, u32[]{:S(2)}, u32[]{:S(2)}) %collective-permute-start.20) | collective-permute-done | bytes 4030496 | tf_op jit(solution)/shard_map/ppermute | solution.py:69
  2838.7 21.1 collective-permute-done.21.refs_1_
  2862.3 31.3 %collective-permute-done.11 = f32[256,1536]{1,0:T(8,128)} collective-permute-done((f32[256,1536]{1,0:T(8,128)}, f32[256,1536]{1,0:T(8,128)}, u32[]{:S(2)}, u32[]{:S(2)}) %collective-permute-start.11) | collective-permute-done | bytes 1572896 | tf_op jit(solution)/shard_map/ppermute | solution.py:69
  2893.5 27.8 collective-permute-done.12
  (288 shorter events, 490.4 us)
Async XLA Ops:
  7.2 341.0 %all-gather.5.cloned.1.call-start = ((), (), s32[]{:S(2)}) async-start(), calls=%async_computation.2 | async-start | bytes 15728640 | tf_op jit(solution)/shard_map/all_gather | solution.py:79
  48.7 2450.8 %reduce-scatter.5.cloned.1.call-start = ((), (), s32[]{:S(2)}) async-start(), calls=%async_computation.4 | async-start | bytes 15728640 | tf_op jit(solution)/shard_map/reduce_scatter | solution.py:134
  52.8 1181.1 %collective-permute-start.10 = (bf16[384,1536]{1,0:T(8,128)(2,1)}, bf16[384,1536]{1,0:T(8,128)(2,1)}, u32[]{:S(2)}, u32[]{:S(2)}) collective-permute-start(bf16[384,1536]{1,0:T(8,128)(2,1)} %get-tuple-element.124), channel_id=1, source_target_pairs={{0,4},{4,0},{1,5},{5,1},{2,6},{6,2},{3,7},{7,3}} | collective-permute-start | bytes 3538952 | tf_op jit(solution)/shard_map/ppermute | solution.py:69
  61.9 1155.1 %collective-permute-start.9 = (bf16[1312,1536]{1,0:T(8,128)(2,1)}, bf16[1312,1536]{1,0:T(8,128)(2,1)}, u32[]{:S(2)}, u32[]{:S(2)}) collective-permute-start(bf16[1312,1536]{1,0:T(8,128)(2,1)} %slice_select_fusion.8), channel_id=1, source_target_pairs={{0,4},{4,0},{1,5},{5,1},{2,6},{6,2},{3,7},{7,3}} | collective-permute-start | bytes 12091400 | tf_op jit(solution)/shard_map/ppermute | solution.py:69
  100.6 394.4 %collective-permute-start.4 = (bf16[2560,1536]{1,0:T(8,128)(2,1)}, bf16[2560,1536]{1,0:T(8,128)(2,1)}, u32[]{:S(2)}, u32[]{:S(2)}) collective-permute-start(bf16[2560,1536]{1,0:T(8,128)(2,1)} %get-tuple-element.125), channel_id=1, source_target_pairs={{0,4},{4,0},{1,5},{5,1},{2,6},{6,2},{3,7},{7,3}} | collective-permute-start | bytes 23592968 | tf_op jit(solution)/shard_map/ppermute | solution.py:69
  102.7 234.2 %collective-permute-start.3 = (s32[256]{0:T(256)S(1)}, s32[256]{0:T(256)S(1)}, u32[]{:S(2)}, u32[]{:S(2)}) collective-permute-start(s32[256]{0:T(256)S(1)} %copy-done.37), channel_id=1, source_target_pairs={{0,4},{4,0},{1,5},{5,1},{2,6},{6,2},{3,7},{7,3}} | collective-permute-start | bytes 3080 | tf_op jit(solution)/shard_map/ppermute | solution.py:69
  108.1 369.2 %collective-permute-start.2 = (bf16[1152,1536]{1,0:T(8,128)(2,1)}, bf16[1152,1536]{1,0:T(8,128)(2,1)}, u32[]{:S(2)}, u32[]{:S(2)}) collective-permute-start(bf16[1152,1536]{1,0:T(8,128)(2,1)} %slice_select_fusion.9), channel_id=1, source_target_pairs={{0,4},{4,0},{1,5},{5,1},{2,6},{6,2},{3,7},{7,3}} | collective-permute-start | bytes 10616840 | tf_op jit(solution)/shard_map/ppermute | solution.py:69
  336.9 132.5 %collective-permute-start.1 = (bf16[384,1536]{1,0:T(8,128)(2,1)}, bf16[384,1536]{1,0:T(8,128)(2,1)}, u32[]{:S(2)}, u32[]{:S(2)}) collective-permute-start(bf16[384,1536]{1,0:T(8,128)(2,1)} %get-tuple-element.123), channel_id=1, source_target_pairs={{0,4},{4,0},{1,5},{5,1},{2,6},{6,2},{3,7},{7,3}} | collective-permute-start | bytes 3538952 | tf_op jit(solution)/shard_map/ppermute | solution.py:69
  469.4 711.3 %collective-permute-start.8 = (bf16[2560,1536]{1,0:T(8,128)(2,1)}, bf16[2560,1536]{1,0:T(8,128)(2,1)}, u32[]{:S(2)}, u32[]{:S(2)}) collective-permute-start(bf16[2560,1536]{1,0:T(8,128)(2,1)} %get-tuple-element.127), channel_id=1, source_target_pairs={{0,4},{4,0},{1,5},{5,1},{2,6},{6,2},{3,7},{7,3}} | collective-permute-start | bytes 23592968 | tf_op jit(solution)/shard_map/ppermute | solution.py:69
  477.3 333.0 %collective-permute-start.5 = (bf16[2560,1536]{1,0:T(8,128)(2,1)}, bf16[2560,1536]{1,0:T(8,128)(2,1)}, u32[]{:S(2)}, u32[]{:S(2)}) collective-permute-start(bf16[2560,1536]{1,0:T(8,128)(2,1)} %get-tuple-element.126), channel_id=1, source_target_pairs={{0,4},{4,0},{1,5},{5,1},{2,6},{6,2},{3,7},{7,3}} | collective-permute-start | bytes 23592968 | tf_op jit(solution)/shard_map/ppermute | solution.py:69
  495.1 483.8 %collective-permute-start.6 = (bf16[2560,1536]{1,0:T(8,128)(2,1)}, bf16[2560,1536]{1,0:T(8,128)(2,1)}, u32[]{:S(2)}, u32[]{:S(2)}) collective-permute-start(bf16[2560,1536]{1,0:T(8,128)(2,1)} %get-tuple-element.129), channel_id=1, source_target_pairs={{0,4},{4,0},{1,5},{5,1},{2,6},{6,2},{3,7},{7,3}} | collective-permute-start | bytes 23592968 | tf_op jit(solution)/shard_map/ppermute | solution.py:69
  810.3 334.2 %collective-permute-start.7 = (bf16[2560,1536]{1,0:T(8,128)(2,1)}, bf16[2560,1536]{1,0:T(8,128)(2,1)}, u32[]{:S(2)}, u32[]{:S(2)}) collective-permute-start(bf16[2560,1536]{1,0:T(8,128)(2,1)} %get-tuple-element.128), channel_id=1, source_target_pairs={{0,4},{4,0},{1,5},{5,1},{2,6},{6,2},{3,7},{7,3}} | collective-permute-start | bytes 23592968 | tf_op jit(solution)/shard_map/ppermute | solution.py:69
  1678.8 823.9 %reduce-scatter.3.cloned.1.call-start = ((), (), s32[]{:S(2)}) async-start(), calls=%async_computation.3 | async-start | bytes 15728640 | tf_op jit(solution)/shard_map/reduce_scatter | solution.py:132
  1798.8 777.4 %collective-permute-start.15 = (bf16[2560,1536]{1,0:T(8,128)(2,1)}, bf16[2560,1536]{1,0:T(8,128)(2,1)}, u32[]{:S(2)}, u32[]{:S(2)}) collective-permute-start(bf16[2560,1536]{1,0:T(8,128)(2,1)} %convolution_convert_fusion.5), channel_id=1, source_target_pairs={{0,4},{4,0},{1,5},{5,1},{2,6},{6,2},{3,7},{7,3}} | collective-permute-start | bytes 23592968 | tf_op jit(solution)/shard_map/ppermute | solution.py:69
  1799.6 778.2 %collective-permute-start.16 = (bf16[2560,1536]{1,0:T(8,128)(2,1)}, bf16[2560,1536]{1,0:T(8,128)(2,1)}, u32[]{:S(2)}, u32[]{:S(2)}) collective-permute-start(bf16[2560,1536]{1,0:T(8,128)(2,1)} %convolution_convert_fusion.4), channel_id=1, source_target_pairs={{0,4},{4,0},{1,5},{5,1},{2,6},{6,2},{3,7},{7,3}} | collective-permute-start | bytes 23592968 | tf_op jit(solution)/shard_map/ppermute | solution.py:69
  1800.9 777.4 %collective-permute-start.17 = (bf16[2560,1536]{1,0:T(8,128)(2,1)}, bf16[2560,1536]{1,0:T(8,128)(2,1)}, u32[]{:S(2)}, u32[]{:S(2)}) collective-permute-start(bf16[2560,1536]{1,0:T(8,128)(2,1)} %convolution_convert_fusion.3), channel_id=1, source_target_pairs={{0,4},{4,0},{1,5},{5,1},{2,6},{6,2},{3,7},{7,3}} | collective-permute-start | bytes 23592968 | tf_op jit(solution)/shard_map/ppermute | solution.py:69
  1801.7 778.2 %collective-permute-start.18 = (bf16[2560,1536]{1,0:T(8,128)(2,1)}, bf16[2560,1536]{1,0:T(8,128)(2,1)}, u32[]{:S(2)}, u32[]{:S(2)}) collective-permute-start(bf16[2560,1536]{1,0:T(8,128)(2,1)} %convolution_convert_fusion.2), channel_id=1, source_target_pairs={{0,4},{4,0},{1,5},{5,1},{2,6},{6,2},{3,7},{7,3}} | collective-permute-start | bytes 23592968 | tf_op jit(solution)/shard_map/ppermute | solution.py:69
  1802.9 696.2 %collective-permute-start.13 = (bf16[384,1536]{1,0:T(8,128)(2,1)S(1)}, bf16[384,1536]{1,0:T(8,128)(2,1)}, u32[]{:S(2)}, u32[]{:S(2)}) collective-permute-start(bf16[384,1536]{1,0:T(8,128)(2,1)S(1)} %copy-done.38), channel_id=1, source_target_pairs={{0,4},{4,0},{1,5},{5,1},{2,6},{6,2},{3,7},{7,3}} | collective-permute-start | bytes 3538952 | tf_op jit(solution)/shard_map/ppermute | solution.py:69
  2499.1 76.7 %collective-permute-start.14 = (bf16[1152,1536]{1,0:T(8,128)(2,1)}, bf16[1152,1536]{1,0:T(8,128)(2,1)S(1)}, u32[]{:S(2)}, u32[]{:S(2)}) collective-permute-start(bf16[1152,1536]{1,0:T(8,128)(2,1)} %convolution_convert_fusion.7), channel_id=1, source_target_pairs={{0,4},{4,0},{1,5},{5,1},{2,6},{6,2},{3,7},{7,3}} | collective-permute-start | bytes 10616840 | tf_op jit(solution)/shard_map/ppermute | solution.py:69
  2575.8 181.9 %collective-permute-start.19 = (bf16[2560,1536]{1,0:T(8,128)(2,1)}, bf16[2560,1536]{1,0:T(8,128)(2,1)}, u32[]{:S(2)}, u32[]{:S(2)}) collective-permute-start(bf16[2560,1536]{1,0:T(8,128)(2,1)} %convolution_convert_fusion.1), channel_id=1, source_target_pairs={{0,4},{4,0},{1,5},{5,1},{2,6},{6,2},{3,7},{7,3}} | collective-permute-start | bytes 23592968 | tf_op jit(solution)/shard_map/ppermute | solution.py:69
  2576.2 258.3 %collective-permute-start.20 = (bf16[1312,1536]{1,0:T(8,128)(2,1)}, bf16[1312,1536]{1,0:T(8,128)(2,1)}, u32[]{:S(2)}, u32[]{:S(2)}) collective-permute-start(bf16[1312,1536]{1,0:T(8,128)(2,1)} %convolution_convert_fusion.6), channel_id=1, source_target_pairs={{0,4},{4,0},{1,5},{5,1},{2,6},{6,2},{3,7},{7,3}} | collective-permute-start | bytes 12091400 | tf_op jit(solution)/shard_map/ppermute | solution.py:69
  2577.8 282.0 %collective-permute-start.21 = (bf16[384,1536]{1,0:T(8,128)(2,1)}, bf16[384,1536]{1,0:T(8,128)(2,1)}, u32[]{:S(2)}, u32[]{:S(2)}) collective-permute-start(bf16[384,1536]{1,0:T(8,128)(2,1)} %convolution_convert_fusion.8), channel_id=1, source_target_pairs={{0,4},{4,0},{1,5},{5,1},{2,6},{6,2},{3,7},{7,3}} | collective-permute-start | bytes 3538952 | tf_op jit(solution)/shard_map/ppermute | solution.py:69
  2578.2 315.3 %collective-permute-start.11 = (f32[256,1536]{1,0:T(8,128)}, f32[256,1536]{1,0:T(8,128)}, u32[]{:S(2)}, u32[]{:S(2)}) collective-permute-start(f32[256,1536]{1,0:T(8,128)} %slice_select_fusion.10), channel_id=1, source_target_pairs={{0,4},{4,0},{1,5},{5,1},{2,6},{6,2},{3,7},{7,3}} | collective-permute-start | bytes 4718600 | tf_op jit(solution)/shard_map/ppermute | solution.py:69
  2579.8 341.5 %collective-permute-start.12 = (f32[256,1536]{1,0:T(8,128)}, f32[256,1536]{1,0:T(8,128)}, u32[]{:S(2)}, u32[]{:S(2)}) collective-permute-start(f32[256,1536]{1,0:T(8,128)} %slice_select_fusion.11), channel_id=1, source_target_pairs={{0,4},{4,0},{1,5},{5,1},{2,6},{6,2},{3,7},{7,3}} | collective-permute-start | bytes 4718600 | tf_op jit(solution)/shard_map/ppermute | solution.py:69
  (70 other events, 2285.8 us)
Sparse Core Ops, SparseCore 0:
  48.9 80.4 all-gather.4
  1678.9 94.0 reduce-scatter.4
  1798.9 93.6 reduce-scatter.2

commit v2 on v1

--- a/solution.py
+++ b/solution.py
@@ -1,13 +1,18 @@
+import functools
+
 import jax
 import jax.numpy as jnp
 from jax import lax
 from jax.experimental import pallas as pl
+from jax.experimental.layout import Layout, with_layout_constraint
 from jax.experimental.pallas import tpu as pltpu
 from jax.sharding import PartitionSpec as P
 
 
-CHUNKS = (384, 1152, 2560, 2560, 2560, 2560, 2560, 1312, 384)
+CHUNKS = (256, 1408, 2560, 2560, 2560, 2560, 2560, 1312, 256)
 SWAP = [(0, 1), (1, 0)]
+SWAP_X = [(0, 2), (2, 0), (1, 3), (3, 1)]
+SWAP_CORE = [(0, 1), (1, 0), (2, 3), (3, 2)]
 
 
 def _place_body(start_ref, *refs):
@@ -44,6 +49,67 @@
     )(jnp.reshape(start, (1,)).astype(jnp.int32), *args)
 
 
+def _stats_body(n_f, n_t, mine, res, slots, send_sems, recv_sems):
+    dp, f, t = lax.axis_index("dp"), lax.axis_index("fsdp"), lax.axis_index("tp")
+    me = f * n_t + t
+    peers = [
+        (dp, lax.rem(f + j // n_t, n_f), lax.rem(t + j % n_t, n_t)) for j in range(1, n_f * n_t)
+    ]
+    barrier = pltpu.get_barrier_semaphore()
+    for peer in peers:
+        pl.semaphore_signal(barrier, inc=1, device_id=peer, device_id_type=pl.DeviceIdType.MESH)
+    pl.semaphore_wait(barrier, len(peers))
+    copies = []
+    for j, peer in enumerate(peers):
+        copy = pltpu.make_async_remote_copy(
+            src_ref=mine,
+            dst_ref=slots.at[me],
+            send_sem=send_sems.at[j],
+            recv_sem=recv_sems.at[j],
+            device_id=peer,
+            device_id_type=pl.DeviceIdType.MESH,
+        )
+        copy.start()
+        copies.append(copy)
+    slots[me] = mine[...]
+    for copy in copies:
+        copy.wait()
+    m = slots[0, 0:1]
+    for d in range(1, n_f * n_t):
+        m = jnp.maximum(m, slots[d, 0:1])
+    s, t_sum = jnp.zeros_like(m), jnp.zeros_like(m)
+    for d in range(n_f * n_t):
+        s += slots[d, 1:2] * jnp.exp(slots[d, 0:1] - m)
+        t_sum += slots[d, 2:3]
+    res[0:1] = m
+    res[1:2] = s
+    res[2:3] = t_sum
+
+
+def combine_stats(mine, n_f, n_t):
+    n = n_f * n_t
+    return pl.pallas_call(
+        functools.partial(_stats_body, n_f, n_t),
+        out_shape=jax.ShapeDtypeStruct(mine.shape, mine.dtype),
+        in_specs=[pl.BlockSpec(memory_space=pltpu.VMEM)],
+        out_specs=pl.BlockSpec(memory_space=pltpu.VMEM),
+        scratch_shapes=[
+            pltpu.VMEM((n,) + mine.shape, mine.dtype),
+            pltpu.SemaphoreType.DMA((n - 1,)),
+            pltpu.SemaphoreType.DMA((n - 1,)),
+        ],
+        compiler_params=pltpu.CompilerParams(
+            collective_id=0, has_side_effects=True, vmem_limit_bytes=4 * 2**20
+        ),
+        cost_estimate=pl.CostEstimate(flops=mine.size * 64, bytes_accessed=mine.size * 64, transcendentals=0),
+        name="stats",
+    )(mine)
+
+
+def row_major(a):
+    return with_layout_constraint(a, Layout(major_to_minor=(0, 1)))
+
+
 def dot_f32(a, b, contract):
     return lax.dot_general(a, b, (contract, ((), ())), preferred_element_type=jnp.float32)
 
@@ -71,20 +137,41 @@
         def pick(a, b):
             return jnp.where(is0, a, b)
 
+        tp_id = lax.axis_index("tp")
+
+        def pick_x(a, b):
+            return jnp.where(tp_id < 2, a, b)
+
+        def pick_c(a, b):
+            return jnp.where(tp_id % 2 == 0, a, b)
+
+        def scatter(a):
+            half_rows = a.shape[0] // 2
+            lo, hi = a[:half_rows], a[half_rows:]
+            got = lax.ppermute(pick_c(hi, lo), "tp", SWAP_CORE)
+            a = pick_c(lo, hi) + got
+            lo, hi = a[: half_rows // 2], a[half_rows // 2 :]
+            got = lax.ppermute(pick_x(hi, lo), "tp", SWAP_X)
+            return pick_x(lo, hi) + got
+
         hid_peer = swap(hidden)
         lab_peer = swap(labels)
         hid2 = jnp.concatenate([pick(hidden, hid_peer), pick(hid_peer, hidden)], axis=0)
         lab2 = jnp.concatenate([pick(labels, lab_peer), pick(lab_peer, labels)], axis=0)
+        hid_x = lax.ppermute(hid2, "tp", SWAP_X)
+        hid4 = jnp.concatenate([pick_x(hid2, hid_x), pick_x(hid_x, hid2)], axis=0)
+        hid_c = lax.ppermute(hid4, "tp", SWAP_CORE)
+        x_full = jnp.concatenate([pick_c(hid4, hid_c), pick_c(hid_c, hid4)], axis=0)
         lab = lax.all_gather(lab2, "tp", axis=0, tiled=True)
-        x_full = lax.all_gather(hid2, "tp", axis=0, tiled=True)
+        lab = lab.reshape(2, 2, -1).transpose(1, 0, 2).reshape(-1)
         x_lo, x_hi = x_full[:, :rows_w], x_full[:, rows_w:]
         x_own, x_oth = pick(x_lo, x_hi), pick(x_hi, x_lo)
 
-        wt = w_head.T
+        wt = row_major(w_head.T)
         oth = []
         for k, width in enumerate(CHUNKS):
             lo, hi = wt[offs[k] : offs[k] + width], wt[half + offs[k] : half + offs[k] + width]
-            oth.append(swap(pick(hi, lo)))
+            oth.append(row_major(swap(row_major(pick(hi, lo)))))
         own = pick(wt[:half], wt[half:])
 
         ids0 = lab - lax.axis_index("tp") * vocab_dev - f * half
@@ -107,10 +194,8 @@
             t = t_new if m is None else t + t_new
             m = m_new
             zs.append(z)
-        stats = lax.all_gather(jnp.stack([m, s, t]), ("fsdp", "tp"), axis=0)
-        row_max = jnp.max(stats[:, 0], axis=0)
-        row_sum = jnp.sum(stats[:, 1] * jnp.exp(stats[:, 0] - row_max[None, :]), axis=0)
-        target = jnp.sum(stats[:, 2], axis=0)
+        stats = combine_stats(jnp.stack([m, s, t]), fsdp_size, tp_size)
+        row_max, row_sum, target = stats[0], stats[1], stats[2]
         tok_loss = row_max + jnp.log(row_sum) - target
         mean_loss = jnp.sum(tok_loss) * inv_tokens
 
@@ -128,10 +213,10 @@
         gs, oth, _ = lax.optimization_barrier((gs, oth, part))
         g_all = jnp.concatenate(gs, axis=0)
         oth_all = jnp.concatenate(oth, axis=0)
-        dx_own = dot_f32(g_all, own, ((0,), (0,)))
-        rs_own = lax.psum_scatter(dx_own, "tp", scatter_dimension=0, tiled=True)
-        dx_oth = dot_f32(g_all, oth_all, ((0,), (0,)))
-        rs_oth = lax.psum_scatter(dx_oth, "tp", scatter_dimension=0, tiled=True)
+        dx_own = row_major(dot_f32(g_all, own, ((0,), (0,))))
+        rs_own = scatter(dx_own)
+        dx_oth = row_major(dot_f32(g_all, oth_all, ((0,), (0,))))
+        rs_oth = scatter(dx_oth)
         dw_own = dot_f32(g_all, x_own, ((1,), (0,))).astype(jnp.bfloat16)
 
         def mine(a):

time: 2940 us -> 3020 us (1.027)
  other arithmetic: 192 us -> 253 us
    ppermute x0 -> x6, waiting for transfers between devices: none -> 174 us  [the longest x2 111 us: scatter(): got = lax.ppermute(pick_x(hi, lo), 'tp', SWAP_X)]
    ppermute x22, waiting for transfers between devices: 1720 us -> 1560 us  [swap(): return lax.ppermute(a, 'fsdp', SWAP)]
    select_n x0 -> x6, other arithmetic: none -> 33.1 us  [the longest x3 23.5 us: pick_c(): return jnp.where(tp_id % 2 == 0, a, b)]
    unnamed x154 -> x179, local copies, waits for them, and re-layouts: 115 us -> 123 us
  transfers between devices with their start and end apart: 25 -> 28, of which waited for: 11 -> 14; matrix products, arithmetic and copies ran while one was open for 22% -> 23% of each run, Pallas kernels for 3% -> 3%
where the time goes in v2:
time: 3020 us
  waiting for transfers between devices  1740 us (58%)
  matrix products  770 us (25%)
  other arithmetic  253 us (8%)
  local copies, waits for them, and re-layouts  126 us (4%)
  Pallas kernels  82.2 us (3%)
  starting transfers between devices  33.5 us (1%)
    ppermute x22, waiting for transfers between devices, swap(): return lax.ppermute(a, 'fsdp', SWAP)  1560 us
    dot_general x22, matrix products, dot_f32(): lax.dot_general(a, b, (contract, ((), ())), preferred_element_type=jnp.fl...  770 us
    unnamed x179, local copies, waits for them, and re-layouts  123 us
    ppermute x2, waiting for transfers between devices, scatter(): got = lax.ppermute(pick_x(hi, lo), 'tp', SWAP_X)  111 us
    pallas_call x10, Pallas kernels, place(): pl.pallas_call(_place_body, out_shape=jax.ShapeDtypeStruct(shape, piece.d...  75.7 us
    select_n x9, other arithmetic, pick(): return jnp.where(is0, a, b)  63.1 us
    ppermute x1, waiting for transfers between devices, inner(): hid_x = lax.ppermute(hid2, 'tp', SWAP_X)  63 us
  transfers between devices with their start and end apart: 28, of which 14 were waited for; matrix products, arithmetic and copies ran while one was open for 23% of the time, Pallas kernels for 3%

profile of v2, /device:TPU:0, one launch (start us, length us, event | category | flops | bytes accessed | tf_op | source)
XLA Modules:
  0.0 3016.0 jit_solution(4178617153200109601)
XLA Ops:
  4.0 34.6 %collective-permute-done = bf16[256,3072]{1,0:T(8,128)(2,1)S(1)} collective-permute-done((bf16[256,3072]{1,0:T(8,128)(2,1)}, bf16[256,3072]{1,0:T(8,128)(2,1)S(1)}, u32[]{:S(2)}, u32[]{:S(2)}) %collective-permute-start) | collective-permute-done | bytes 1572896 | tf_op jit(solution)/shard_map/ppermute | solution.py:135
  48.2 63.0 %collective-permute-done.1 = bf16[512,3072]{1,0:T(8,128)(2,1)} collective-permute-done((bf16[512,3072]{1,0:T(8,128)(2,1)S(1)}, bf16[512,3072]{1,0:T(8,128)(2,1)}, u32[]{:S(2)}, u32[]{:S(2)}) %collective-permute-start.1) | collective-permute-done | bytes 3145760 | tf_op jit(solution)/shard_map/ppermute | solution.py:161
  125.3 37.8 %slice_select_fusion.5 = (bf16[2560,1536]{1,0:T(8,128)(2,1)}, bf16[2560,1536]{1,0:T(8,128)(2,1)}, bf16[2560,1536]{1,0:T(8,128)(2,1)}, bf16[2560,1536]{1,0:T(8,128)(2,1)}, bf16[2560,1536]{1,0:T(8,128)(2,1)}) fusion(bf16[32064,1536]{1,0:T(8,128)(2,1)} %bitcast, pred[]{:T(512)S(6)} %eq.65), kind=kLoop, calls=%fused_computation.62 | loop fusion | flops 19660800 | bytes 117964800 | tf_op jit(solution)/shard_map/jit(_where)/select_n | solution.py:138
  171.3 210.9 %collective-permute-done.5 = s32[256]{0:T(256)S(1)} collective-permute-done((s32[256]{0:T(256)S(1)}, s32[256]{0:T(256)S(1)}, u32[]{:S(2)}, u32[]{:S(2)}) %collective-permute-start.5) | collective-permute-done | bytes 1056 | tf_op jit(solution)/shard_map/ppermute | solution.py:135
  408.9 114.3 %fusion.15 = f32[16032,2048]{1,0:T(8,128)} fusion(bf16[32064,1536]{1,0:T(8,128)(2,1)} %bitcast, pred[]{:T(512)S(6)} %eq.65, bf16[2048,1536]{1,0:T(8,128)(2,1)} %broadcast_select_fusion.17), kind=kOutput, calls=%fused_computation.66 | convolution fusion | flops 100889247744 | bytes 236126208 | tf_op jit(solution)/shard_map/dot_general | solution.py:114
  560.5 26.1 fusion.27
  596.6 273.4 %collective-permute-done.7 = bf16[2560,1536]{1,0:T(8,128)(2,1)} collective-permute-done((bf16[2560,1536]{1,0:T(8,128)(2,1)}, bf16[2560,1536]{1,0:T(8,128)(2,1)}, u32[]{:S(2)}, u32[]{:S(2)}) %collective-permute-start.7) | collective-permute-done | bytes 7864352 | tf_op jit(solution)/shard_map/ppermute | solution.py:135
  871.5 26.3 fusion.28
  907.9 130.7 %collective-permute-done.8 = bf16[2560,1536]{1,0:T(8,128)(2,1)} collective-permute-done((bf16[2560,1536]{1,0:T(8,128)(2,1)}, bf16[2560,1536]{1,0:T(8,128)(2,1)}, u32[]{:S(2)}, u32[]{:S(2)}) %collective-permute-start.8) | collective-permute-done | bytes 7864352 | tf_op jit(solution)/shard_map/ppermute | solution.py:135
  1038.5 26.0 fusion.29
  1074.6 129.4 %collective-permute-done.9 = bf16[2560,1536]{1,0:T(8,128)(2,1)} collective-permute-done((bf16[2560,1536]{1,0:T(8,128)(2,1)}, bf16[2560,1536]{1,0:T(8,128)(2,1)}, u32[]{:S(2)}, u32[]{:S(2)}) %collective-permute-start.9) | collective-permute-done | bytes 7864352 | tf_op jit(solution)/shard_map/ppermute | solution.py:135
  1204.0 26.2 fusion.30
  1240.2 26.0 fusion.31
  1366.9 23.1 convolution_convert_fusion.4
  1619.2 114.7 %fusion.33 = f32[2048,1536]{1,0:T(8,128)} fusion(bf16[16032,2048]{1,0:T(8,128)(2,1)} %constant_dynamic-update-slice_fusion, bf16[16032,1536]{1,0:T(8,128)(2,1)} %constant_dynamic-update-slice_fusion.9), kind=kOutput, calls=%fused_computation.165 | convolution fusion | flops 100864622592 | bytes 127500288 | tf_op jit(solution)/shard_map/dot_general | solution.py:114
  1742.8 116.8 %fusion.14 = f32[2048,1536]{1,0:T(8,128)} fusion(bf16[16032,2048]{1,0:T(8,128)(2,1)} %constant_dynamic-update-slice_fusion, bf16[32064,1536]{1,0:T(8,128)(2,1)} %bitcast, pred[]{:T(512)S(6)} %eq.65), kind=kOutput, calls=%fused_computation.65 | convolution fusion | flops 100889247744 | bytes 176750592 | tf_op jit(solution)/shard_map/dot_general | solution.py:114
  1907.1 43.4 %collective-permute-done.16 = f32[512,1536]{1,0:T(8,128)} collective-permute-done((f32[512,1536]{1,0:T(8,128)}, f32[512,1536]{1,0:T(8,128)}, u32[]{:S(2)}, u32[]{:S(2)}) %collective-permute-start.16) | collective-permute-done | bytes 3145760 | tf_op jit(solution)/shard_map/ppermute | solution.py:154
  1951.9 67.9 %collective-permute-done.14 = f32[512,1536]{1,0:T(8,128)} collective-permute-done((f32[512,1536]{1,0:T(8,128)S(1)}, f32[512,1536]{1,0:T(8,128)}, u32[]{:S(2)}, u32[]{:S(2)}) %collective-permute-start.14) | collective-permute-done | bytes 3145760 | tf_op jit(solution)/shard_map/ppermute | solution.py:154
  2033.0 634.9 %collective-permute-done.20.refs_1_ = bf16[1408,1536]{1,0:T(8,128)(2,1)} collective-permute-done((bf16[1408,1536]{1,0:T(8,128)(2,1)}, bf16[1408,1536]{1,0:T(8,128)(2,1)}, u32[]{:S(2)}, u32[]{:S(2)}) %collective-permute-start.20) | collective-permute-done | bytes 4325408 | tf_op jit(solution)/shard_map/ppermute | solution.py:135
  2673.4 113.5 %convolution_convert_fusion.refs_0_ = bf16[16032,1536]{1,0:T(8,128)(2,1)} fusion(bf16[16032,2048]{1,0:T(8,128)(2,1)} %constant_dynamic-update-slice_fusion, pred[]{:T(512)S(6)} %eq.65, bf16[1024,3072]{1,0:T(8,128)(2,1)} %copy-done.2, bf16[1024,3072]{1,0:T(8,128)(2,1)} %copy-done.1), kind=kOutput, calls=%fused_computation | convolution fusion | flops 100917559296 | bytes 127500288 | tf_op jit(solution)/shard_map/dot_general | solution.py:114
  2788.2 33.1 %place.10.refs_0_ = bf16[32064,1536]{1,0:T(8,128)(2,1)} custom-call(s32[1]{0:T(128)} %bitcast.19.start_ref, bf16[16032,1536]{1,0:T(8,128)(2,1)} %convolution_convert_fusion.refs_0_), custom_call_target="tpu_custom_call" | custom-call | flops 98500608 | bytes 98500608 | tf_op jit(solution)/shard_map/place/pallas_call | solution.py:36
  2857.7 69.0 %collective-permute-done.26.refs_1_ = bf16[1312,1536]{1,0:T(8,128)(2,1)} collective-permute-done((bf16[1312,1536]{1,0:T(8,128)(2,1)}, bf16[1312,1536]{1,0:T(8,128)(2,1)}, u32[]{:S(2)}, u32[]{:S(2)}) %collective-permute-start.26) | collective-permute-done | bytes 4030496 | tf_op jit(solution)/shard_map/ppermute | solution.py:135
  2945.7 31.5 %collective-permute-done.17 = f32[256,1536]{1,0:T(8,128)} collective-permute-done((f32[256,1536]{1,0:T(8,128)}, f32[256,1536]{1,0:T(8,128)}, u32[]{:S(2)}, u32[]{:S(2)}) %collective-permute-start.17) | collective-permute-done | bytes 1572896 | tf_op jit(solution)/shard_map/ppermute | solution.py:135
  2977.3 31.8 %collective-permute-done.18 = f32[256,1536]{1,0:T(8,128)} collective-permute-done((f32[256,1536]{1,0:T(8,128)}, f32[256,1536]{1,0:T(8,128)}, u32[]{:S(2)}, u32[]{:S(2)}) %collective-permute-start.18) | collective-permute-done | bytes 1572896 | tf_op jit(solution)/shard_map/ppermute | solution.py:135
  (332 shorter events, 607.2 us)
Async XLA Ops:
  46.7 1247.0 %collective-permute-start.12 = (bf16[256,1536]{1,0:T(8,128)(2,1)}, bf16[256,1536]{1,0:T(8,128)(2,1)}, u32[]{:S(2)}, u32[]{:S(2)}) collective-permute-start(bf16[256,1536]{1,0:T(8,128)(2,1)} %get-tuple-element.126), channel_id=1, source_target_pairs={{0,4},{4,0},{1,5},{5,1},{2,6},{6,2},{3,7},{7,3}} | collective-permute-start | bytes 2359304 | tf_op jit(solution)/shard_map/ppermute | solution.py:135
  118.1 274.6 %collective-permute-start.2 = (bf16[1024,3072]{1,0:T(8,128)(2,1)}, bf16[1024,3072]{1,0:T(8,128)(2,1)}, u32[]{:S(2)}, u32[]{:S(2)}) collective-permute-start(bf16[1024,3072]{1,0:T(8,128)(2,1)} %pad_maximum_fusion.1), channel_id=1, source_target_pairs={{0,1},{1,0},{2,3},{3,2},{4,5},{5,4},{6,7},{7,6}} | collective-permute-start | bytes 18874376 | tf_op jit(solution)/shard_map/ppermute | solution.py:163
  123.8 1152.5 %collective-permute-start.11 = (bf16[1312,1536]{1,0:T(8,128)(2,1)}, bf16[1312,1536]{1,0:T(8,128)(2,1)}, u32[]{:S(2)}, u32[]{:S(2)}) collective-permute-start(bf16[1312,1536]{1,0:T(8,128)(2,1)} %slice_select_fusion.11), channel_id=1, source_target_pairs={{0,4},{4,0},{1,5},{5,1},{2,6},{6,2},{3,7},{7,3}} | collective-permute-start | bytes 12091400 | tf_op jit(solution)/shard_map/ppermute | solution.py:135
  163.1 396.5 %collective-permute-start.6 = (bf16[2560,1536]{1,0:T(8,128)(2,1)}, bf16[2560,1536]{1,0:T(8,128)(2,1)}, u32[]{:S(2)}, u32[]{:S(2)}) collective-permute-start(bf16[2560,1536]{1,0:T(8,128)(2,1)} %get-tuple-element.127), channel_id=1, source_target_pairs={{0,4},{4,0},{1,5},{5,1},{2,6},{6,2},{3,7},{7,3}} | collective-permute-start | bytes 23592968 | tf_op jit(solution)/shard_map/ppermute | solution.py:135
  163.7 218.4 %collective-permute-start.5 = (s32[256]{0:T(256)S(1)}, s32[256]{0:T(256)S(1)}, u32[]{:S(2)}, u32[]{:S(2)}) collective-permute-start(s32[256]{0:T(256)S(1)} %copy-done.44), channel_id=1, source_target_pairs={{0,4},{4,0},{1,5},{5,1},{2,6},{6,2},{3,7},{7,3}} | collective-permute-start | bytes 3080 | tf_op jit(solution)/shard_map/ppermute | solution.py:135
  382.2 153.2 %collective-permute-start.4 = (bf16[1408,1536]{1,0:T(8,128)(2,1)}, bf16[1408,1536]{1,0:T(8,128)(2,1)}, u32[]{:S(2)}, u32[]{:S(2)}) collective-permute-start(bf16[1408,1536]{1,0:T(8,128)(2,1)} %slice_select_fusion.10), channel_id=1, source_target_pairs={{0,4},{4,0},{1,5},{5,1},{2,6},{6,2},{3,7},{7,3}} | collective-permute-start | bytes 12976136 | tf_op jit(solution)/shard_map/ppermute | solution.py:135
  392.7 136.3 %collective-permute-start.3 = (bf16[256,1536]{1,0:T(8,128)(2,1)}, bf16[256,1536]{1,0:T(8,128)(2,1)}, u32[]{:S(2)}, u32[]{:S(2)}) collective-permute-start(bf16[256,1536]{1,0:T(8,128)(2,1)} %get-tuple-element.125), channel_id=1, source_target_pairs={{0,4},{4,0},{1,5},{5,1},{2,6},{6,2},{3,7},{7,3}} | collective-permute-start | bytes 2359304 | tf_op jit(solution)/shard_map/ppermute | solution.py:135
  529.1 711.2 %collective-permute-start.10 = (bf16[2560,1536]{1,0:T(8,128)(2,1)}, bf16[2560,1536]{1,0:T(8,128)(2,1)}, u32[]{:S(2)}, u32[]{:S(2)}) collective-permute-start(bf16[2560,1536]{1,0:T(8,128)(2,1)} %get-tuple-element.130), channel_id=1, source_target_pairs={{0,4},{4,0},{1,5},{5,1},{2,6},{6,2},{3,7},{7,3}} | collective-permute-start | bytes 23592968 | tf_op jit(solution)/shard_map/ppermute | solution.py:135
  535.4 334.6 %collective-permute-start.7 = (bf16[2560,1536]{1,0:T(8,128)(2,1)}, bf16[2560,1536]{1,0:T(8,128)(2,1)}, u32[]{:S(2)}, u32[]{:S(2)}) collective-permute-start(bf16[2560,1536]{1,0:T(8,128)(2,1)} %get-tuple-element.128), channel_id=1, source_target_pairs={{0,4},{4,0},{1,5},{5,1},{2,6},{6,2},{3,7},{7,3}} | collective-permute-start | bytes 23592968 | tf_op jit(solution)/shard_map/ppermute | solution.py:135
  559.7 478.8 %collective-permute-start.8 = (bf16[2560,1536]{1,0:T(8,128)(2,1)}, bf16[2560,1536]{1,0:T(8,128)(2,1)}, u32[]{:S(2)}, u32[]{:S(2)}) collective-permute-start(bf16[2560,1536]{1,0:T(8,128)(2,1)} %get-tuple-element.131), channel_id=1, source_target_pairs={{0,4},{4,0},{1,5},{5,1},{2,6},{6,2},{3,7},{7,3}} | collective-permute-start | bytes 23592968 | tf_op jit(solution)/shard_map/ppermute | solution.py:135
  870.0 333.9 %collective-permute-start.9 = (bf16[2560,1536]{1,0:T(8,128)(2,1)}, bf16[2560,1536]{1,0:T(8,128)(2,1)}, u32[]{:S(2)}, u32[]{:S(2)}) collective-permute-start(bf16[2560,1536]{1,0:T(8,128)(2,1)} %get-tuple-element.129), channel_id=1, source_target_pairs={{0,4},{4,0},{1,5},{5,1},{2,6},{6,2},{3,7},{7,3}} | collective-permute-start | bytes 23592968 | tf_op jit(solution)/shard_map/ppermute | solution.py:135
  1742.7 126.1 %collective-permute-start.15 = (f32[1024,1536]{1,0:T(8,128)}, f32[1024,1536]{1,0:T(8,128)}, u32[]{:S(2)}, u32[]{:S(2)}) collective-permute-start(f32[1024,1536]{1,0:T(8,128)} %slice_select_fusion.8), channel_id=1, source_target_pairs={{0,1},{1,0},{2,3},{3,2},{4,5},{5,4},{6,7},{7,6}} | collective-permute-start | bytes 18874376 | tf_op jit(solution)/shard_map/ppermute | solution.py:151
  1880.0 70.5 %collective-permute-start.16 = (f32[512,1536]{1,0:T(8,128)}, f32[512,1536]{1,0:T(8,128)}, u32[]{:S(2)}, u32[]{:S(2)}) collective-permute-start(f32[512,1536]{1,0:T(8,128)} %slice_select_fusion.12), channel_id=1, source_target_pairs={{0,2},{2,0},{1,3},{3,1},{4,6},{6,4},{5,7},{7,5}} | collective-permute-start | bytes 9437192 | tf_op jit(solution)/shard_map/ppermute | solution.py:154
  1882.9 786.5 %collective-permute-start.21 = (bf16[2560,1536]{1,0:T(8,128)(2,1)}, bf16[2560,1536]{1,0:T(8,128)(2,1)}, u32[]{:S(2)}, u32[]{:S(2)}) collective-permute-start(bf16[2560,1536]{1,0:T(8,128)(2,1)} %convolution_convert_fusion.5), channel_id=1, source_target_pairs={{0,4},{4,0},{1,5},{5,1},{2,6},{6,2},{3,7},{7,3}} | collective-permute-start | bytes 23592968 | tf_op jit(solution)/shard_map/ppermute | solution.py:135
  1883.5 786.5 %collective-permute-start.22 = (bf16[2560,1536]{1,0:T(8,128)(2,1)}, bf16[2560,1536]{1,0:T(8,128)(2,1)}, u32[]{:S(2)}, u32[]{:S(2)}) collective-permute-start(bf16[2560,1536]{1,0:T(8,128)(2,1)} %convolution_convert_fusion.4), channel_id=1, source_target_pairs={{0,4},{4,0},{1,5},{5,1},{2,6},{6,2},{3,7},{7,3}} | collective-permute-start | bytes 23592968 | tf_op jit(solution)/shard_map/ppermute | solution.py:135
  1884.9 786.5 %collective-permute-start.23 = (bf16[2560,1536]{1,0:T(8,128)(2,1)}, bf16[2560,1536]{1,0:T(8,128)(2,1)}, u32[]{:S(2)}, u32[]{:S(2)}) collective-permute-start(bf16[2560,1536]{1,0:T(8,128)(2,1)} %convolution_convert_fusion.3), channel_id=1, source_target_pairs={{0,4},{4,0},{1,5},{5,1},{2,6},{6,2},{3,7},{7,3}} | collective-permute-start | bytes 23592968 | tf_op jit(solution)/shard_map/ppermute | solution.py:135
  1902.2 769.8 %collective-permute-start.24 = (bf16[2560,1536]{1,0:T(8,128)(2,1)}, bf16[2560,1536]{1,0:T(8,128)(2,1)}, u32[]{:S(2)}, u32[]{:S(2)}) collective-permute-start(bf16[2560,1536]{1,0:T(8,128)(2,1)} %convolution_convert_fusion.2), channel_id=1, source_target_pairs={{0,4},{4,0},{1,5},{5,1},{2,6},{6,2},{3,7},{7,3}} | collective-permute-start | bytes 23592968 | tf_op jit(solution)/shard_map/ppermute | solution.py:135
  1950.4 69.4 %collective-permute-start.14 = (f32[512,1536]{1,0:T(8,128)S(1)}, f32[512,1536]{1,0:T(8,128)}, u32[]{:S(2)}, u32[]{:S(2)}) collective-permute-start(f32[512,1536]{1,0:T(8,128)S(1)} %slice_select_fusion.13), channel_id=1, source_target_pairs={{0,2},{2,0},{1,3},{3,1},{4,6},{6,4},{5,7},{7,5}} | collective-permute-start | bytes 9437192 | tf_op jit(solution)/shard_map/ppermute | solution.py:154
  2019.9 648.1 %collective-permute-start.20 = (bf16[1408,1536]{1,0:T(8,128)(2,1)}, bf16[1408,1536]{1,0:T(8,128)(2,1)}, u32[]{:S(2)}, u32[]{:S(2)}) collective-permute-start(bf16[1408,1536]{1,0:T(8,128)(2,1)} %convolution_convert_fusion.7), channel_id=1, source_target_pairs={{0,4},{4,0},{1,5},{5,1},{2,6},{6,2},{3,7},{7,3}} | collective-permute-start | bytes 12976136 | tf_op jit(solution)/shard_map/ppermute | solution.py:135
  2667.9 183.8 %collective-permute-start.25 = (bf16[2560,1536]{1,0:T(8,128)(2,1)}, bf16[2560,1536]{1,0:T(8,128)(2,1)}, u32[]{:S(2)}, u32[]{:S(2)}) collective-permute-start(bf16[2560,1536]{1,0:T(8,128)(2,1)} %convolution_convert_fusion.1), channel_id=1, source_target_pairs={{0,4},{4,0},{1,5},{5,1},{2,6},{6,2},{3,7},{7,3}} | collective-permute-start | bytes 23592968 | tf_op jit(solution)/shard_map/ppermute | solution.py:135
  2669.4 257.3 %collective-permute-start.26 = (bf16[1312,1536]{1,0:T(8,128)(2,1)}, bf16[1312,1536]{1,0:T(8,128)(2,1)}, u32[]{:S(2)}, u32[]{:S(2)}) collective-permute-start(bf16[1312,1536]{1,0:T(8,128)(2,1)} %convolution_convert_fusion.6), channel_id=1, source_target_pairs={{0,4},{4,0},{1,5},{5,1},{2,6},{6,2},{3,7},{7,3}} | collective-permute-start | bytes 12091400 | tf_op jit(solution)/shard_map/ppermute | solution.py:135
  2670.0 273.6 %collective-permute-start.27 = (bf16[256,1536]{1,0:T(8,128)(2,1)}, bf16[256,1536]{1,0:T(8,128)(2,1)}, u32[]{:S(2)}, u32[]{:S(2)}) collective-permute-start(bf16[256,1536]{1,0:T(8,128)(2,1)} %convolution_convert_fusion.8), channel_id=1, source_target_pairs={{0,4},{4,0},{1,5},{5,1},{2,6},{6,2},{3,7},{7,3}} | collective-permute-start | bytes 2359304 | tf_op jit(solution)/shard_map/ppermute | solution.py:135
  2671.4 305.9 %collective-permute-start.17 = (f32[256,1536]{1,0:T(8,128)}, f32[256,1536]{1,0:T(8,128)}, u32[]{:S(2)}, u32[]{:S(2)}) collective-permute-start(f32[256,1536]{1,0:T(8,128)} %slice_select_fusion.14), channel_id=1, source_target_pairs={{0,4},{4,0},{1,5},{5,1},{2,6},{6,2},{3,7},{7,3}} | collective-permute-start | bytes 4718600 | tf_op jit(solution)/shard_map/ppermute | solution.py:135
  2672.0 337.1 %collective-permute-start.18 = (f32[256,1536]{1,0:T(8,128)}, f32[256,1536]{1,0:T(8,128)}, u32[]{:S(2)}, u32[]{:S(2)}) collective-permute-start(f32[256,1536]{1,0:T(8,128)} %slice_select_fusion.15), channel_id=1, source_target_pairs={{0,4},{4,0},{1,5},{5,1},{2,6},{6,2},{3,7},{7,3}} | collective-permute-start | bytes 4718600 | tf_op jit(solution)/shard_map/ppermute | solution.py:135
  (85 other events, 2461.9 us)
